TPU v7x, 32 devices: a whole 2x2x4 slice. The times are simulated.
32 devices in a mesh: seq: 16 (over z, y, core), head: 2 (over x).
Axes of the slice: x: 2, y: 2, z: 4, core: 2. Of those that a mesh axis runs over, the one named last changes fastest.
Arguments:
- tokens: bfloat16 [8192, 1024], P('seq'), may hold values from -24 to 24
- norm_attn: float32 [1024], replicated, may hold values from 0.5 to 1.5
- self_qkv: bfloat16 [3, 1024, 1024], P(None, None, 'head'), may hold values from -4 to 4
- self_out: bfloat16 [1024, 1024], P('head'), may hold values from -0.1875 to 0.1875
- norm_ffn: float32 [1024], replicated, may hold values from 0.5 to 1.5
- ffn_in: bfloat16 [2, 1024, 2816], P(None, None, 'head'), may hold values from -0.1875 to 0.1875
- ffn_out: bfloat16 [2816, 1024], P('head'), may hold values from -0.109375 to 0.109375
- norm_final: float32 [1024], replicated, may hold values from 0.5 to 1.5
- pad_lengths: int32 [16], replicated, may hold values from 64 to 512
- targets: bfloat16 [512, 1024], replicated, may hold values from -8 to 8
- target_lengths: int32 [4], replicated, may hold values from 32 to 128
- norm_cross: float32 [1024], replicated, may hold values from 0.1 to 1.9
- cross_query: bfloat16 [1024, 1024], P(None, 'head'), may hold values from -4 to 4
- cross_kv: bfloat16 [2, 1024, 1024], P(None, None, 'head'), may hold values from -4 to 4
- cross_out: bfloat16 [1024, 1024], P('head'), may hold values from -4 to 4
Outputs:
- encoded: bfloat16 [8192, 1024], P('seq')
- decoded: bfloat16 [512, 1024], replicated
All inputs are finite; a program needn't handle non-finite values.
Results may differ from a plain program's by a relative error of at most 0.033.
Values may be sent and summed in bfloat16 or wider, within the bound.
A program may use at most 128 MiB of HBM per device.

v0:
```python
import math
import jax
import jax.numpy as jnp
from jax import lax
from jax.sharding import PartitionSpec as P

HD = 64
TOK_DEV = 512
TGT_LEN = 128
epsilon = 1e-06
masked_score = -1e30


def rms_norm(values, gain_vector):
    widened = values.astype(jnp.float32)
    return (
        widened
        * lax.rsqrt(jnp.mean(widened * widened, axis=-1, keepdims=True) + epsilon)
        * gain_vector
    )


def spread_heads(per_head):
    return jnp.repeat(per_head.T, HD, axis=1)


def live_within(positions, lengths, span):
    block_ids = jnp.arange(lengths.shape[0], dtype=jnp.int32)
    owners = positions // span
    lengths_here = jnp.sum(
        jnp.where(owners[:, None] == block_ids[None, :], lengths[None, :], 0), axis=1
    )
    return positions % span < lengths_here


def live_keys(positions, pad_lengths):
    return live_within(positions, pad_lengths, TOK_DEV)


def flash_block(flash_state, query_heads, key_rows, value_rows, live_rows, scaling):
    running_max, running_sum, running_acc = flash_state
    key_count = key_rows.shape[0]
    heads_here = query_heads.shape[1]
    keys_split = key_rows.reshape(key_count, heads_here, HD)
    values_split = value_rows.reshape(key_count, heads_here, HD)
    scores = (
        jnp.einsum("qhd,khd->hqk", query_heads, keys_split, preferred_element_type=jnp.float32)
        * scaling
    )
    scores = jnp.where(live_rows[None, None, :], scores, masked_score)
    new_max = jnp.maximum(running_max, jnp.max(scores, axis=-1))
    shrink = jnp.exp(running_max - new_max)
    weights = jnp.where(live_rows[None, None, :], jnp.exp(scores - new_max[:, :, None]), 0.0)
    new_sum = running_sum * shrink + jnp.sum(weights, axis=-1)
    mixed_values = jnp.einsum(
        "hqk,khd->qhd",
        weights.astype(jnp.bfloat16),
        values_split,
        preferred_element_type=jnp.float32,
    )
    new_acc = running_acc * spread_heads(shrink) + mixed_values.reshape(
        mixed_values.shape[0], heads_here * HD
    )
    return (new_max, new_sum, new_acc)


def feed_forward(normed_in, ffn_in, ffn_out):
    gate_proj = jnp.dot(normed_in, ffn_in[0], preferred_element_type=jnp.float32)
    up_proj = jnp.dot(normed_in, ffn_in[1], preferred_element_type=jnp.float32)
    activated = (jax.nn.gelu(gate_proj, approximate=True) * up_proj).astype(jnp.bfloat16)
    return jnp.dot(activated, ffn_out, preferred_element_type=jnp.float32)


def local(
    tokens,
    norm_attn,
    self_qkv,
    self_out,
    norm_ffn,
    ffn_in,
    ffn_out,
    norm_final,
    pad_lengths,
    targets,
    target_lengths,
    norm_cross,
    cross_query,
    cross_kv,
    cross_out,
):
    row_count = tokens.shape[0]
    heads_here = self_qkv.shape[2] // HD
    scaling = HD ** (-0.5)
    normed = rms_norm(tokens, norm_attn).astype(jnp.bfloat16)
    queries = jnp.dot(normed, self_qkv[0], preferred_element_type=jnp.float32).astype(jnp.bfloat16)
    keys_local = jnp.dot(normed, self_qkv[1], preferred_element_type=jnp.float32).astype(
        jnp.bfloat16
    )
    values_local = jnp.dot(normed, self_qkv[2], preferred_element_type=jnp.float32).astype(
        jnp.bfloat16
    )
    query_heads = queries.reshape(row_count, heads_here, HD)
    start_state = (
        jnp.full((heads_here, row_count), masked_score, jnp.float32),
        jnp.zeros((heads_here, row_count), jnp.float32),
        jnp.zeros((row_count, heads_here * HD), jnp.float32),
    )
    key_piece = lax.all_gather(keys_local, "seq", axis=0, tiled=True)
    value_piece = lax.all_gather(values_local, "seq", axis=0, tiled=True)
    piece_rows = key_piece.shape[0]
    block_width = math.gcd(piece_rows, 2048)

    def step_once(inner_state, block_index):
        first_row = block_index * block_width
        key_rows = lax.dynamic_slice_in_dim(key_piece, first_row, block_width, 0)
        value_rows = lax.dynamic_slice_in_dim(value_piece, first_row, block_width, 0)
        positions = first_row + jnp.arange(block_width, dtype=jnp.int32)
        updated = flash_block(
            inner_state,
            query_heads,
            key_rows,
            value_rows,
            live_keys(positions, pad_lengths),
            scaling,
        )
        return (updated, None)

    final_state, unused = lax.scan(
        step_once, start_state, jnp.arange(piece_rows // block_width, dtype=jnp.int32)
    )
    final_max, final_sum, final_acc = final_state
    context = (final_acc / spread_heads(final_sum)).astype(jnp.bfloat16)
    attn_part = jnp.dot(context, self_out, preferred_element_type=jnp.float32)
    hidden_in = tokens.astype(jnp.float32) + lax.psum(
        attn_part.astype(jnp.bfloat16), "head"
    ).astype(jnp.float32)
    ffn_normed = rms_norm(hidden_in, norm_ffn).astype(jnp.bfloat16)
    ffn_part = feed_forward(ffn_normed, ffn_in, ffn_out)
    final_in = hidden_in + lax.psum(ffn_part.astype(jnp.bfloat16), "head").astype(jnp.float32)
    encoded = rms_norm(final_in, norm_final).astype(jnp.bfloat16)
    target_rows = targets.shape[0]
    cross_normed = rms_norm(targets, norm_cross).astype(jnp.bfloat16)
    cross_queries = jnp.dot(cross_normed, cross_query, preferred_element_type=jnp.float32).astype(
        jnp.bfloat16
    )
    cross_keys = jnp.dot(encoded, cross_kv[0], preferred_element_type=jnp.float32).astype(
        jnp.bfloat16
    )
    cross_values = jnp.dot(encoded, cross_kv[1], preferred_element_type=jnp.float32).astype(
        jnp.bfloat16
    )
    cross_heads = cross_queries.reshape(target_rows, heads_here, HD)
    keys_split = cross_keys.reshape(row_count, heads_here, HD)
    values_split = cross_values.reshape(row_count, heads_here, HD)
    positions = lax.axis_index("seq") * row_count + jnp.arange(row_count, dtype=jnp.int32)
    live_here = live_keys(positions, pad_lengths)
    cross_scores = (
        jnp.einsum("qhd,khd->hqk", cross_heads, keys_split, preferred_element_type=jnp.float32)
        * scaling
    )
    cross_scores = jnp.where(live_here[None, None, :], cross_scores, masked_score)
    local_max = jnp.max(cross_scores, axis=-1)
    global_max = lax.pmax(local_max, "seq")
    weights = jnp.where(
        live_here[None, None, :], jnp.exp(cross_scores - global_max[:, :, None]), 0.0
    )
    local_sum = jnp.sum(weights, axis=-1)
    local_mixed = jnp.einsum(
        "hqk,khd->qhd",
        weights.astype(jnp.bfloat16),
        values_split,
        preferred_element_type=jnp.float32,
    )
    weight_sum, mixed_values = (
        lax.psum(local_sum.astype(jnp.bfloat16), "seq").astype(jnp.float32),
        lax.psum(
            local_mixed.reshape(target_rows, heads_here * HD).astype(jnp.bfloat16), "seq"
        ).astype(jnp.float32),
    )
    cross_context = (mixed_values / spread_heads(weight_sum)).astype(jnp.bfloat16)
    cross_part = jnp.dot(cross_context, cross_out, preferred_element_type=jnp.float32)
    cross_total = lax.psum(cross_part.astype(jnp.bfloat16), "head").astype(jnp.float32)
    slots = jnp.arange(target_rows, dtype=jnp.int32)
    target_live = slots % TGT_LEN < jnp.repeat(
        target_lengths, TGT_LEN, total_repeat_length=target_rows
    )
    decoded = (
        targets.astype(jnp.float32) + jnp.where(target_live[:, None], cross_total, 0.0)
    ).astype(jnp.bfloat16)
    return (encoded, decoded)


def solution(mesh):
    placed = (
        P("seq", None),
        P(),
        P(None, None, "head"),
        P("head", None),
        P(),
        P(None, None, "head"),
        P("head", None),
        P(),
        P(),
        P(),
        P(),
        P(),
        P(None, "head"),
        P(None, None, "head"),
        P("head", None),
    )
    return jax.shard_map(
        local, mesh=mesh, in_specs=placed, out_specs=(P("seq", None), P()), check_vma=False
    )
```

profile of v0, /device:TPU:0, one launch (start us, length us, event | category | flops | bytes accessed | tf_op | source)
XLA Modules:
  0.0 726.6 jit_solution(55890220503606311)
XLA Ops:
  17.7 71.5 %all-gather.3.cloned.1.call-done = bf16[8192,512]{1,0:T(8,128)(2,1)} async-done(((bf16[512,512]{1,0:T(8,128)(2,1)}), bf16[8192,512]{1,0:T(8,128)(2,1)}) %all-gather.3.cloned.1.call-update) | async-done | bytes 8388624 | tf_op jit(solution)/shard_map/all_gather | solution.py:108
  89.2 75.1 %all-gather.5.cloned.1.call-done = bf16[8192,512]{1,0:T(8,128)(2,1)} async-done(((bf16[512,512]{1,0:T(8,128)(2,1)}), bf16[8192,512]{1,0:T(8,128)(2,1)}) %all-gather.5.cloned.1.call-update) | async-done | bytes 8388624 | tf_op jit(solution)/shard_map/all_gather | solution.py:109
  164.3 242.0 %while.18 = (s32[]{:T(128)}, f32[8,512]{1,0:T(8,128)S(1)}, f32[8,512]{1,0:T(8,128)S(1)}, f32[512,512]{0,1:T(8,128)}, s32[4]{0:T(128)S(1)}, /*index=5*/s32[16]{0:...) while((s32[]{:T(128)}, f32[8,512]{1,0:T(8,128)S(1)}, ...), condition=%wide.region_5.6_spmd.clone, body=%wide.region_1.5_spmd.clone.sunk | while | flops 2257502208 | bytes 135045456 | solution.py:128
  174.1 15.6 %bitcast_reduce_fusion.2 = (f32[8,512]{1,0:T(8,128)S(1)}, f32[8,2048,512]{2,1,0:T(8,128)}) fusion(pred[2048]{0:T(1024)(128)(4,1)S(1)} %fusion.113, bf16[2048,8,64]{0,2,1:T(8,128)(2,1)} %bitcast.120, bf16[512,8,64]{0,2,1:T(8,128)(2,1)S(1)} %get-tuple-element.311), kind=kOutput, calls=%fused_computation.1.clone.1 | convolution fusion | flops 1098903552 | bytes 36194304 | tf_op jit(solution)/shard_map/while/body/eval_jaxpr/qhd,khd->hqk/dot_general | solution.py:47
  193.7 14.9 %fusion.117 = f32[8,64,512]{2,1,0:T(8,128)S(1)} fusion(bf16[2048,8,64]{0,2,1:T(8,128)(2,1)} %bitcast.121, f32[8,2048,512]{2,1,0:T(8,128)} %get-tuple-element.275, f32[8,512]{1,0:T(8,128)S(1)} %get-tuple-element.305, pred[2048]{0:T(1024)(128)(4,1)S(1)} %fusion.113), kind=kOutput, calls=%fused_computation.7.clone.1 | convolution fusion | flops 1115684864 | bytes 36718592 | tf_op jit(solution)/shard_map/while/body/eval_jaxpr/hqk,khd->qhd/dot_general | solution.py:55
  209.0 15.7 %fusion.115 = f32[8,512]{1,0:T(8,128)S(1)} fusion(f32[8,2048,512]{2,1,0:T(8,128)} %get-tuple-element.275, f32[8,512]{1,0:T(8,128)S(1)} %get-tuple-element.305, pred[2048]{0:T(1024)(128)(4,1)S(1)} %fusion.113), kind=kLoop, calls=%fused_computation.6.clone.1 | loop fusion | flops 41938944 | bytes 33589248 | tf_op jit(solution)/shard_map/while/body/eval_jaxpr/reduce_sum | solution.py:54
  234.6 15.6 %bitcast_reduce_fusion.2 = (f32[8,512]{1,0:T(8,128)S(1)}, f32[8,2048,512]{2,1,0:T(8,128)}) fusion(pred[2048]{0:T(1024)(128)(4,1)S(1)} %fusion.113, bf16[2048,8,64]{0,2,1:T(8,128)(2,1)} %bitcast.120, bf16[512,8,64]{0,2,1:T(8,128)(2,1)S(1)} %get-tuple-element.311), kind=kOutput, calls=%fused_computation.1.clone.1 | convolution fusion | flops 1098903552 | bytes 36194304 | tf_op jit(solution)/shard_map/while/body/eval_jaxpr/qhd,khd->hqk/dot_general | solution.py:47
  254.2 14.9 %fusion.117 = f32[8,64,512]{2,1,0:T(8,128)S(1)} fusion(bf16[2048,8,64]{0,2,1:T(8,128)(2,1)} %bitcast.121, f32[8,2048,512]{2,1,0:T(8,128)} %get-tuple-element.275, f32[8,512]{1,0:T(8,128)S(1)} %get-tuple-element.305, pred[2048]{0:T(1024)(128)(4,1)S(1)} %fusion.113), kind=kOutput, calls=%fused_computation.7.clone.1 | convolution fusion | flops 1115684864 | bytes 36718592 | tf_op jit(solution)/shard_map/while/body/eval_jaxpr/hqk,khd->qhd/dot_general | solution.py:55
  269.5 15.7 %fusion.115 = f32[8,512]{1,0:T(8,128)S(1)} fusion(f32[8,2048,512]{2,1,0:T(8,128)} %get-tuple-element.275, f32[8,512]{1,0:T(8,128)S(1)} %get-tuple-element.305, pred[2048]{0:T(1024)(128)(4,1)S(1)} %fusion.113), kind=kLoop, calls=%fused_computation.6.clone.1 | loop fusion | flops 41938944 | bytes 33589248 | tf_op jit(solution)/shard_map/while/body/eval_jaxpr/reduce_sum | solution.py:54
  295.1 15.6 %bitcast_reduce_fusion.2 = (f32[8,512]{1,0:T(8,128)S(1)}, f32[8,2048,512]{2,1,0:T(8,128)}) fusion(pred[2048]{0:T(1024)(128)(4,1)S(1)} %fusion.113, bf16[2048,8,64]{0,2,1:T(8,128)(2,1)} %bitcast.120, bf16[512,8,64]{0,2,1:T(8,128)(2,1)S(1)} %get-tuple-element.311), kind=kOutput, calls=%fused_computation.1.clone.1 | convolution fusion | flops 1098903552 | bytes 36194304 | tf_op jit(solution)/shard_map/while/body/eval_jaxpr/qhd,khd->hqk/dot_general | solution.py:47
  314.7 14.9 %fusion.117 = f32[8,64,512]{2,1,0:T(8,128)S(1)} fusion(bf16[2048,8,64]{0,2,1:T(8,128)(2,1)} %bitcast.121, f32[8,2048,512]{2,1,0:T(8,128)} %get-tuple-element.275, f32[8,512]{1,0:T(8,128)S(1)} %get-tuple-element.305, pred[2048]{0:T(1024)(128)(4,1)S(1)} %fusion.113), kind=kOutput, calls=%fused_computation.7.clone.1 | convolution fusion | flops 1115684864 | bytes 36718592 | tf_op jit(solution)/shard_map/while/body/eval_jaxpr/hqk,khd->qhd/dot_general | solution.py:55
  330.1 15.7 %fusion.115 = f32[8,512]{1,0:T(8,128)S(1)} fusion(f32[8,2048,512]{2,1,0:T(8,128)} %get-tuple-element.275, f32[8,512]{1,0:T(8,128)S(1)} %get-tuple-element.305, pred[2048]{0:T(1024)(128)(4,1)S(1)} %fusion.113), kind=kLoop, calls=%fused_computation.6.clone.1 | loop fusion | flops 41938944 | bytes 33589248 | tf_op jit(solution)/shard_map/while/body/eval_jaxpr/reduce_sum | solution.py:54
  355.7 15.6 %bitcast_reduce_fusion.2 = (f32[8,512]{1,0:T(8,128)S(1)}, f32[8,2048,512]{2,1,0:T(8,128)}) fusion(pred[2048]{0:T(1024)(128)(4,1)S(1)} %fusion.113, bf16[2048,8,64]{0,2,1:T(8,128)(2,1)} %bitcast.120, bf16[512,8,64]{0,2,1:T(8,128)(2,1)S(1)} %get-tuple-element.311), kind=kOutput, calls=%fused_computation.1.clone.1 | convolution fusion | flops 1098903552 | bytes 36194304 | tf_op jit(solution)/shard_map/while/body/eval_jaxpr/qhd,khd->hqk/dot_general | solution.py:47
  375.3 14.9 %fusion.117 = f32[8,64,512]{2,1,0:T(8,128)S(1)} fusion(bf16[2048,8,64]{0,2,1:T(8,128)(2,1)} %bitcast.121, f32[8,2048,512]{2,1,0:T(8,128)} %get-tuple-element.275, f32[8,512]{1,0:T(8,128)S(1)} %get-tuple-element.305, pred[2048]{0:T(1024)(128)(4,1)S(1)} %fusion.113), kind=kOutput, calls=%fused_computation.7.clone.1 | convolution fusion | flops 1115684864 | bytes 36718592 | tf_op jit(solution)/shard_map/while/body/eval_jaxpr/hqk,khd->qhd/dot_general | solution.py:55
  390.6 15.7 %fusion.115 = f32[8,512]{1,0:T(8,128)S(1)} fusion(f32[8,2048,512]{2,1,0:T(8,128)} %get-tuple-element.275, f32[8,512]{1,0:T(8,128)S(1)} %get-tuple-element.305, pred[2048]{0:T(1024)(128)(4,1)S(1)} %fusion.113), kind=kLoop, calls=%fused_computation.6.clone.1 | loop fusion | flops 41938944 | bytes 33589248 | tf_op jit(solution)/shard_map/while/body/eval_jaxpr/reduce_sum | solution.py:54
  410.9 38.6 %all-reduce.5.cloned.1.call-done = bf16[512,1024]{1,0:T(8,128)(2,1)} async-done(((bf16[512,1024]{1,0:T(8,128)(2,1)}), bf16[512,1024]{1,0:T(8,128)(2,1)}) %all-reduce.5.cloned.1.call-update) | async-done | bytes 1048592 | tf_op jit(solution)/shard_map/psum | solution.py:134
  451.5 5.9 fusion.34
  457.4 7.9 %convolution_convert_fusion = bf16[512,1024]{1,0:T(8,128)(2,1)} fusion(bf16[1408,1024]{1,0:T(8,128)(2,1)S(1)} %copy-done, f32[512,1408]{1,0:T(8,128)} %fusion.34, bf16[2,1024,1408]{2,1,0:T(8,128)(2,1)} %param.24, bf16[512,1024]{1,0:T(8,128)(2,1)} %all-reduce.5.cloned.1.call-done, bf16[512,1024]{1,0:T(8,128)(2,1)} %param.19, f32[1024]{0:T(1024)S(1)} %copy-done.12, ...), kind=kOutput, calls=%fused_computation.77 | convolution fusion | flops 2963668992 | bytes 11802624 | tf_op jit(solution)/shard_map/dot_general | solution.py:71
  469.4 36.1 %all-reduce.7.cloned.1.call-done = bf16[512,1024]{1,0:T(8,128)(2,1)} async-done(((bf16[512,1024]{1,0:T(8,128)(2,1)}), bf16[512,1024]{1,0:T(8,128)(2,1)}) %all-reduce.7.cloned.1.call-update) | async-done | bytes 1048592 | tf_op jit(solution)/shard_map/psum | solution.py:139
  517.2 61.0 %pmax.7 = f32[8,512]{1,0:T(8,128)S(1)} all-reduce(f32[8,512]{1,0:T(8,128)S(1)} %get-tuple-element.209), channel_id=1, replica_groups=mesh['seq'=16,'head'=2] {'seq'}, use_global_device_ids=true, to_apply=%region_13.14 | all-reduce | flops 4096 | bytes 32768 | tf_op jit(solution)/shard_map/pmax | solution.py:163
  578.2 6.4 fusion.45
  589.4 30.1 %psum.38 = bf16[512,8]{0,1:T(8,128)(2,1)S(1)} all-reduce(bf16[512,8]{0,1:T(8,128)(2,1)S(1)} %bitcast.127), channel_id=1, replica_groups=mesh['seq'=16,'head'=2] {'seq'}, use_global_device_ids=true, to_apply=%region_16.17 | all-reduce | flops 4096 | bytes 16384 | tf_op jit(solution)/shard_map/psum | solution.py:175
  619.6 52.5 %all-reduce.9.cloned.1.call-done = bf16[512,512]{0,1:T(8,128)(2,1)} async-done(((bf16[512,512]{0,1:T(8,128)(2,1)}), bf16[512,512]{0,1:T(8,128)(2,1)}) %all-reduce.9.cloned.1.call-update) | async-done | bytes 524304 | tf_op jit(solution)/shard_map/psum | solution.py:176
  679.4 37.5 %all-reduce.11.cloned.1.call-done = bf16[512,1024]{1,0:T(8,128)(2,1)} async-done(((bf16[512,1024]{1,0:T(8,128)(2,1)}), bf16[512,1024]{1,0:T(8,128)(2,1)}) %all-reduce.11.cloned.1.call-update) | async-done | bytes 1048592 | tf_op jit(solution)/shard_map/psum | solution.py:182
  (131 shorter events, 101.6 us)
Async XLA Ops:
  7.2 450.2 %copy-start = (bf16[1408,1024]{1,0:T(8,128)(2,1)S(1)}, bf16[1408,1024]{1,0:T(8,128)(2,1)}, u32[]{:S(2)}) copy-start(bf16[1408,1024]{1,0:T(8,128)(2,1)} %param.25) | copy-start | bytes 8650756
  7.2 4.9 copy-start.11
  7.2 82.0 %all-gather.3.cloned.1.call-start = ((), (), s32[]{:S(2)}) async-start(), calls=%async_computation | async-start | bytes 8912896 | tf_op jit(solution)/shard_map/all_gather | solution.py:108
  12.0 152.3 %all-gather.5.cloned.1.call-start = ((), (), s32[]{:S(2)}) async-start(), calls=%async_computation.1 | async-start | bytes 8912896 | tf_op jit(solution)/shard_map/all_gather | solution.py:109
  15.2 149.1 %copy-start.7 = (s32[16]{0:T(128)S(1)}, s32[16]{0:T(128)}, u32[]{:S(2)}) copy-start(s32[16]{0:T(128)} %param.27) | copy-start | bytes 196
  15.2 434.3 %all-reduce.5.cloned.1.call-start = ((), (), s32[]{:S(2)}) async-start(), calls=%async_computation.2 | async-start | bytes 2097152 | tf_op jit(solution)/shard_map/psum | solution.py:134
  193.7 14.9 %copy-start.1 = (f32[512,512]{0,1:T(8,128)S(1)}, f32[512,512]{0,1:T(8,128)}, u32[]{:S(2)}) copy-start(f32[512,512]{0,1:T(8,128)} %get-tuple-element.294) | copy-start | bytes 3145732 | tf_op jit(solution)/shard_map/while
  209.0 15.7 %copy-start.2 = (f32[512,512]{0,1:T(8,128)}, f32[512,512]{0,1:T(8,128)S(1)}, u32[]{:S(2)}) copy-start(f32[512,512]{0,1:T(8,128)S(1)} %bitcast_add_fusion.2) | copy-start | bytes 3145732 | tf_op jit(solution)/shard_map/while
  254.2 14.9 %copy-start.1 = (f32[512,512]{0,1:T(8,128)S(1)}, f32[512,512]{0,1:T(8,128)}, u32[]{:S(2)}) copy-start(f32[512,512]{0,1:T(8,128)} %get-tuple-element.294) | copy-start | bytes 3145732 | tf_op jit(solution)/shard_map/while
  269.5 15.7 %copy-start.2 = (f32[512,512]{0,1:T(8,128)}, f32[512,512]{0,1:T(8,128)S(1)}, u32[]{:S(2)}) copy-start(f32[512,512]{0,1:T(8,128)S(1)} %bitcast_add_fusion.2) | copy-start | bytes 3145732 | tf_op jit(solution)/shard_map/while
  314.7 14.9 %copy-start.1 = (f32[512,512]{0,1:T(8,128)S(1)}, f32[512,512]{0,1:T(8,128)}, u32[]{:S(2)}) copy-start(f32[512,512]{0,1:T(8,128)} %get-tuple-element.294) | copy-start | bytes 3145732 | tf_op jit(solution)/shard_map/while
  330.0 15.7 %copy-start.2 = (f32[512,512]{0,1:T(8,128)}, f32[512,512]{0,1:T(8,128)S(1)}, u32[]{:S(2)}) copy-start(f32[512,512]{0,1:T(8,128)S(1)} %bitcast_add_fusion.2) | copy-start | bytes 3145732 | tf_op jit(solution)/shard_map/while
  375.3 14.9 %copy-start.1 = (f32[512,512]{0,1:T(8,128)S(1)}, f32[512,512]{0,1:T(8,128)}, u32[]{:S(2)}) copy-start(f32[512,512]{0,1:T(8,128)} %get-tuple-element.294) | copy-start | bytes 3145732 | tf_op jit(solution)/shard_map/while
  390.6 15.7 %copy-start.2 = (f32[512,512]{0,1:T(8,128)}, f32[512,512]{0,1:T(8,128)S(1)}, u32[]{:S(2)}) copy-start(f32[512,512]{0,1:T(8,128)S(1)} %bitcast_add_fusion.2) | copy-start | bytes 3145732 | tf_op jit(solution)/shard_map/while
  407.7 43.8 %copy-start.12 = (f32[1024]{0:T(1024)S(1)}, f32[1024]{0:T(1024)}, u32[]{:S(2)}) copy-start(f32[1024]{0:T(1024)} %param.23) | copy-start | bytes 12292
  410.6 94.9 %all-reduce.7.cloned.1.call-start = ((), (), s32[]{:S(2)}) async-start(), calls=%async_computation.3 | async-start | bytes 2097152 | tf_op jit(solution)/shard_map/psum | solution.py:139
  457.4 9.6 %copy-start.13 = (f32[1024]{0:T(1024)S(1)}, f32[1024]{0:T(1024)}, u32[]{:S(2)}) copy-start(f32[1024]{0:T(1024)} %param.30) | copy-start | bytes 12292
  465.3 206.8 %all-reduce.9.cloned.1.call-start = ((), (), s32[]{:S(2)}) async-start(), calls=%async_computation.4 | async-start | bytes 1048576 | tf_op jit(solution)/shard_map/psum | solution.py:176
  467.0 41.1 %copy-start.9 = (f32[1024]{0:T(1024)S(1)}, f32[1024]{0:T(1024)}, u32[]{:S(2)}) copy-start(f32[1024]{0:T(1024)} %param.26) | copy-start | bytes 12292
  505.5 2.6 copy-start.3
  505.5 2.6 copy-start.4
  505.5 2.8 copy-start.5
  584.7 132.2 %all-reduce.11.cloned.1.call-start = ((), (), s32[]{:S(2)}) async-start(), calls=%async_computation.5 | async-start | bytes 2097152 | tf_op jit(solution)/shard_map/psum | solution.py:182
  589.4 86.8 %copy-start.8 = (s32[4]{0:T(128)S(1)}, s32[4]{0:T(128)}, u32[]{:S(2)}) copy-start(s32[4]{0:T(128)} %param.29) | copy-start | bytes 52
  (2 other events, 4.0 us)
Sparse Core Ops, SparseCore 0:
  12.2 77.0 all-gather.2
  91.4 72.8 all-gather.4
  410.8 38.6 all-reduce.4
  465.4 40.0 all-reduce.6
  584.8 87.1 all-reduce.8
  676.3 40.5 all-reduce.10
where the time goes:
time: 728 us; the launch traced here: 727 us
  waiting for transfers between devices  311 us (43%)
  matrix products  167 us (23%)
  blocking collectives  91.1 us (13%)
  other arithmetic  85.7 us (12%)
  local copies, waits for them, and re-layouts  53.9 us (7%)
  between operations  14.4 us (2%)
    all_gather x1, waiting for transfers between devices, local(): value_piece = lax.all_gather(values_local, 'seq', axis=0, tiled=True)  75.1 us
    all_gather x1, waiting for transfers between devices, local(): key_piece = lax.all_gather(keys_local, 'seq', axis=0, tiled=True)  71.5 us
    reduce_sum x4, other arithmetic, flash_block(): new_sum = running_sum * shrink + jnp.sum(weights, axis=-1)  62.8 us
    dot_general x4, matrix products, flash_block(): jnp.einsum('qhd,khd->hqk', query_heads, keys_split, preferred_element_typ...  62.5 us
    pmax x1, blocking collectives, local(): global_max = lax.pmax(local_max, 'seq')  61 us
    dot_general x4, matrix products, flash_block(): jnp.einsum('hqk,khd->qhd', weights.astype(jnp.bfloat16), values_split, pr...  59.7 us
    psum x1, waiting for transfers between devices, local(): lax.psum(local_mixed.reshape(target_rows, heads_here * HD).astype(jnp.bfl...  52.5 us
    psum x1, waiting for transfers between devices, local(): lax.psum(attn_part.astype(jnp.bfloat16), 'head').astype(jnp.float32)  38.6 us
  transfers between devices with their start and end apart: 6, of which 6 were waited for; matrix products, arithmetic and copies ran while one was open for 2% of the time, Pallas kernels for 0%

commit v1 on v0

--- a/solution.py
+++ b/solution.py
@@ -105,8 +105,13 @@
         jnp.zeros((heads_here, row_count), jnp.float32),
         jnp.zeros((row_count, heads_here * HD), jnp.float32),
     )
-    key_piece = lax.all_gather(keys_local, "seq", axis=0, tiled=True)
-    value_piece = lax.all_gather(values_local, "seq", axis=0, tiled=True)
+    key_piece, value_piece = jnp.split(
+        lax.all_gather(
+            jnp.concatenate([keys_local, values_local], axis=1), "seq", axis=0, tiled=True
+        ),
+        [keys_local.shape[1]],
+        axis=1,
+    )
     piece_rows = key_piece.shape[0]
     block_width = math.gcd(piece_rows, 2048)
 

time: 728 us -> 683 us (0.938)
  local copies, waits for them, and re-layouts: 53.9 us -> 31.7 us
  waiting for transfers between devices: 311 us -> 295 us
    dynamic_slice x8 -> x4, local copies, waits for them, and re-layouts: 33.8 us -> 15.9 us  [step_once(): lax.dynamic_slice_in_dim(value_piece, first_row, block_width, 0)]
    all_gather x2 -> x1, waiting for transfers between devices: 147 us -> 130 us  [local(): lax.all_gather(jnp.concatenate([keys_local, values_local], axis=1), 'seq'...]
    dynamic_slice x4 -> x0, local copies, waits for them, and re-layouts: 15.9 us -> none  [step_once(): key_rows = lax.dynamic_slice_in_dim(key_piece, first_row, block_width, 0)]
    split x0 -> x1, local copies, waits for them, and re-layouts: none -> 11.6 us  [local(): jnp.split(lax.all_gather(jnp.concatenate([keys_local, values_local], axis...]
  transfers between devices with their start and end apart: 6 -> 5, of which waited for: 6 -> 5; matrix products, arithmetic and copies ran while one was open for 2% -> 2% of each run, Pallas kernels for 0% -> 0%
where the time goes in v1:
time: 683 us; the launch traced here: 682 us
  waiting for transfers between devices  295 us (43%)
  matrix products  160 us (23%)
  blocking collectives  91.1 us (13%)
  other arithmetic  86.8 us (13%)
  local copies, waits for them, and re-layouts  31.7 us (5%)
  between operations  14.1 us (2%)
    all_gather x1, waiting for transfers between devices, local(): lax.all_gather(jnp.concatenate([keys_local, values_local], axis=1), 'seq'...  130 us
    reduce_sum x4, other arithmetic, flash_block(): new_sum = running_sum * shrink + jnp.sum(weights, axis=-1)  62.8 us
    pmax x1, blocking collectives, local(): global_max = lax.pmax(local_max, 'seq')  61 us
    dot_general x4, matrix products, flash_block(): jnp.einsum('hqk,khd->qhd', weights.astype(jnp.bfloat16), values_split, pr...  59.9 us
    dot_general x4, matrix products, flash_block(): jnp.einsum('qhd,khd->hqk', query_heads, keys_split, preferred_element_typ...  57.7 us
    psum x1, waiting for transfers between devices, local(): lax.psum(local_mixed.reshape(target_rows, heads_here * HD).astype(jnp.bfl...  52.5 us
    psum x1, waiting for transfers between devices, local(): lax.psum(attn_part.astype(jnp.bfloat16), 'head').astype(jnp.float32)  38.2 us
    psum x1, waiting for transfers between devices, local(): lax.psum(cross_part.astype(jnp.bfloat16), 'head').astype(jnp.float32)  37.5 us
  transfers between devices with their start and end apart: 5, of which 5 were waited for; matrix products, arithmetic and copies ran while one was open for 2% of the time, Pallas kernels for 0%

profile of v1, /device:TPU:0, one launch (start us, length us, event | category | flops | bytes accessed | tf_op | source)
XLA Modules:
  0.0 682.1 jit_solution(8168460260050811754)
XLA Ops:
  17.0 130.3 %all-gather.2.cloned.1.call-done = bf16[8192,1024]{0,1:T(8,128)(2,1)} async-done(((bf16[512,1024]{0,1:T(8,128)(2,1)}), bf16[8192,1024]{0,1:T(8,128)(2,1)}) %all-gather.2.cloned.1.call-update) | async-done | bytes 16777232 | tf_op jit(solution)/shard_map/all_gather | solution.py:109
  147.3 11.6 %fusion.85 = (bf16[8192,512]{0,1:T(8,128)(2,1)}, bf16[8192,512]{0,1:T(8,128)(2,1)}) fusion(bf16[8192,1024]{0,1:T(8,128)(2,1)} %all-gather.2.cloned.1.call-done), kind=kLoop, calls=%fused_computation.143 | loop fusion | bytes 33554432 | tf_op jit(solution)/shard_map/split | solution.py:108
  158.8 203.7 %while.18 = (s32[]{:T(128)}, f32[8,512]{1,0:T(8,128)S(1)}, f32[8,512]{1,0:T(8,128)S(1)}, f32[512,512]{0,1:T(8,128)}, s32[4]{0:T(128)S(1)}, /*index=5*/s32[16]{0:...) while((s32[]{:T(128)}, f32[8,512]{1,0:T(8,128)S(1)}, ...), condition=%wide.region_5.6_spmd.clone, body=%wide.region_1.5_spmd.clone.sunk | while | flops 2257502208 | bytes 126656840 | solution.py:133
  164.2 14.4 %bitcast_reduce_fusion.2 = (f32[8,512]{1,0:T(8,128)S(1)}, f32[8,2048,512]{2,1,0:T(8,128)}) fusion(pred[2048]{0:T(1024)(128)(4,1)S(1)} %fusion.114, bf16[2048,8,64]{0,2,1:T(8,128)(2,1)S(1)} %bitcast.120, bf16[512,8,64]{0,2,1:T(8,128)(2,1)S(1)} %get-tuple-element.295), kind=kOutput, calls=%fused_computation.1.clone.1 | convolution fusion | flops 1098903552 | bytes 36194304 | tf_op jit(solution)/shard_map/while/body/eval_jaxpr/qhd,khd->hqk/dot_general | solution.py:47
  178.6 15.0 %fusion.118 = f32[8,64,512]{2,1,0:T(8,128)S(1)} fusion(bf16[2048,8,64]{0,2,1:T(8,128)(2,1)} %bitcast.121, f32[8,2048,512]{2,1,0:T(8,128)} %get-tuple-element.259, f32[8,512]{1,0:T(8,128)S(1)} %get-tuple-element.289, pred[2048]{0:T(1024)(128)(4,1)S(1)} %fusion.114), kind=kOutput, calls=%fused_computation.7.clone.1 | convolution fusion | flops 1115684864 | bytes 36718592 | tf_op jit(solution)/shard_map/while/body/eval_jaxpr/hqk,khd->qhd/dot_general | solution.py:55
  194.0 15.7 %fusion.116 = f32[8,512]{1,0:T(8,128)S(1)} fusion(f32[8,2048,512]{2,1,0:T(8,128)} %get-tuple-element.259, f32[8,512]{1,0:T(8,128)S(1)} %get-tuple-element.289, pred[2048]{0:T(1024)(128)(4,1)S(1)} %fusion.114), kind=kLoop, calls=%fused_computation.6.clone.1 | loop fusion | flops 41938944 | bytes 33589248 | tf_op jit(solution)/shard_map/while/body/eval_jaxpr/reduce_sum | solution.py:54
  215.1 14.4 %bitcast_reduce_fusion.2 = (f32[8,512]{1,0:T(8,128)S(1)}, f32[8,2048,512]{2,1,0:T(8,128)}) fusion(pred[2048]{0:T(1024)(128)(4,1)S(1)} %fusion.114, bf16[2048,8,64]{0,2,1:T(8,128)(2,1)S(1)} %bitcast.120, bf16[512,8,64]{0,2,1:T(8,128)(2,1)S(1)} %get-tuple-element.295), kind=kOutput, calls=%fused_computation.1.clone.1 | convolution fusion | flops 1098903552 | bytes 36194304 | tf_op jit(solution)/shard_map/while/body/eval_jaxpr/qhd,khd->hqk/dot_general | solution.py:47
  229.6 15.0 %fusion.118 = f32[8,64,512]{2,1,0:T(8,128)S(1)} fusion(bf16[2048,8,64]{0,2,1:T(8,128)(2,1)} %bitcast.121, f32[8,2048,512]{2,1,0:T(8,128)} %get-tuple-element.259, f32[8,512]{1,0:T(8,128)S(1)} %get-tuple-element.289, pred[2048]{0:T(1024)(128)(4,1)S(1)} %fusion.114), kind=kOutput, calls=%fused_computation.7.clone.1 | convolution fusion | flops 1115684864 | bytes 36718592 | tf_op jit(solution)/shard_map/while/body/eval_jaxpr/hqk,khd->qhd/dot_general | solution.py:55
  244.9 15.7 %fusion.116 = f32[8,512]{1,0:T(8,128)S(1)} fusion(f32[8,2048,512]{2,1,0:T(8,128)} %get-tuple-element.259, f32[8,512]{1,0:T(8,128)S(1)} %get-tuple-element.289, pred[2048]{0:T(1024)(128)(4,1)S(1)} %fusion.114), kind=kLoop, calls=%fused_computation.6.clone.1 | loop fusion | flops 41938944 | bytes 33589248 | tf_op jit(solution)/shard_map/while/body/eval_jaxpr/reduce_sum | solution.py:54
  266.1 14.4 %bitcast_reduce_fusion.2 = (f32[8,512]{1,0:T(8,128)S(1)}, f32[8,2048,512]{2,1,0:T(8,128)}) fusion(pred[2048]{0:T(1024)(128)(4,1)S(1)} %fusion.114, bf16[2048,8,64]{0,2,1:T(8,128)(2,1)S(1)} %bitcast.120, bf16[512,8,64]{0,2,1:T(8,128)(2,1)S(1)} %get-tuple-element.295), kind=kOutput, calls=%fused_computation.1.clone.1 | convolution fusion | flops 1098903552 | bytes 36194304 | tf_op jit(solution)/shard_map/while/body/eval_jaxpr/qhd,khd->hqk/dot_general | solution.py:47
  280.5 15.0 %fusion.118 = f32[8,64,512]{2,1,0:T(8,128)S(1)} fusion(bf16[2048,8,64]{0,2,1:T(8,128)(2,1)} %bitcast.121, f32[8,2048,512]{2,1,0:T(8,128)} %get-tuple-element.259, f32[8,512]{1,0:T(8,128)S(1)} %get-tuple-element.289, pred[2048]{0:T(1024)(128)(4,1)S(1)} %fusion.114), kind=kOutput, calls=%fused_computation.7.clone.1 | convolution fusion | flops 1115684864 | bytes 36718592 | tf_op jit(solution)/shard_map/while/body/eval_jaxpr/hqk,khd->qhd/dot_general | solution.py:55
  295.9 15.7 %fusion.116 = f32[8,512]{1,0:T(8,128)S(1)} fusion(f32[8,2048,512]{2,1,0:T(8,128)} %get-tuple-element.259, f32[8,512]{1,0:T(8,128)S(1)} %get-tuple-element.289, pred[2048]{0:T(1024)(128)(4,1)S(1)} %fusion.114), kind=kLoop, calls=%fused_computation.6.clone.1 | loop fusion | flops 41938944 | bytes 33589248 | tf_op jit(solution)/shard_map/while/body/eval_jaxpr/reduce_sum | solution.py:54
  317.0 14.4 %bitcast_reduce_fusion.2 = (f32[8,512]{1,0:T(8,128)S(1)}, f32[8,2048,512]{2,1,0:T(8,128)}) fusion(pred[2048]{0:T(1024)(128)(4,1)S(1)} %fusion.114, bf16[2048,8,64]{0,2,1:T(8,128)(2,1)S(1)} %bitcast.120, bf16[512,8,64]{0,2,1:T(8,128)(2,1)S(1)} %get-tuple-element.295), kind=kOutput, calls=%fused_computation.1.clone.1 | convolution fusion | flops 1098903552 | bytes 36194304 | tf_op jit(solution)/shard_map/while/body/eval_jaxpr/qhd,khd->hqk/dot_general | solution.py:47
  331.4 15.0 %fusion.118 = f32[8,64,512]{2,1,0:T(8,128)S(1)} fusion(bf16[2048,8,64]{0,2,1:T(8,128)(2,1)} %bitcast.121, f32[8,2048,512]{2,1,0:T(8,128)} %get-tuple-element.259, f32[8,512]{1,0:T(8,128)S(1)} %get-tuple-element.289, pred[2048]{0:T(1024)(128)(4,1)S(1)} %fusion.114), kind=kOutput, calls=%fused_computation.7.clone.1 | convolution fusion | flops 1115684864 | bytes 36718592 | tf_op jit(solution)/shard_map/while/body/eval_jaxpr/hqk,khd->qhd/dot_general | solution.py:55
  346.8 15.7 %fusion.116 = f32[8,512]{1,0:T(8,128)S(1)} fusion(f32[8,2048,512]{2,1,0:T(8,128)} %get-tuple-element.259, f32[8,512]{1,0:T(8,128)S(1)} %get-tuple-element.289, pred[2048]{0:T(1024)(128)(4,1)S(1)} %fusion.114), kind=kLoop, calls=%fused_computation.6.clone.1 | loop fusion | flops 41938944 | bytes 33589248 | tf_op jit(solution)/shard_map/while/body/eval_jaxpr/reduce_sum | solution.py:54
  367.1 38.2 %all-reduce.5.cloned.1.call-done = bf16[512,1024]{1,0:T(8,128)(2,1)} async-done(((bf16[512,1024]{1,0:T(8,128)(2,1)}), bf16[512,1024]{1,0:T(8,128)(2,1)}) %all-reduce.5.cloned.1.call-update) | async-done | bytes 1048592 | tf_op jit(solution)/shard_map/psum | solution.py:139
  407.3 5.9 fusion.34
  413.2 7.9 %convolution_convert_fusion = bf16[512,1024]{1,0:T(8,128)(2,1)} fusion(bf16[1408,1024]{1,0:T(8,128)(2,1)S(1)} %copy-done, f32[512,1408]{1,0:T(8,128)} %fusion.34, bf16[2,1024,1408]{2,1,0:T(8,128)(2,1)} %param.24, bf16[512,1024]{1,0:T(8,128)(2,1)} %all-reduce.5.cloned.1.call-done, bf16[512,1024]{1,0:T(8,128)(2,1)} %param.19, f32[1024]{0:T(1024)S(1)} %copy-done.13, ...), kind=kOutput, calls=%fused_computation.77 | convolution fusion | flops 2963668992 | bytes 11802624 | tf_op jit(solution)/shard_map/dot_general | solution.py:71
  425.2 36.1 %all-reduce.7.cloned.1.call-done = bf16[512,1024]{1,0:T(8,128)(2,1)} async-done(((bf16[512,1024]{1,0:T(8,128)(2,1)}), bf16[512,1024]{1,0:T(8,128)(2,1)}) %all-reduce.7.cloned.1.call-update) | async-done | bytes 1048592 | tf_op jit(solution)/shard_map/psum | solution.py:144
  473.0 61.0 %pmax.7 = f32[8,512]{1,0:T(8,128)S(1)} all-reduce(f32[8,512]{1,0:T(8,128)S(1)} %get-tuple-element.193), channel_id=1, replica_groups=mesh['seq'=16,'head'=2] {'seq'}, use_global_device_ids=true, to_apply=%region_13.14 | all-reduce | flops 4096 | bytes 32768 | tf_op jit(solution)/shard_map/pmax | solution.py:168
  534.1 6.4 fusion.45
  545.3 30.1 %psum.38 = bf16[512,8]{0,1:T(8,128)(2,1)S(1)} all-reduce(bf16[512,8]{0,1:T(8,128)(2,1)S(1)} %bitcast.127), channel_id=1, replica_groups=mesh['seq'=16,'head'=2] {'seq'}, use_global_device_ids=true, to_apply=%region_16.17 | all-reduce | flops 4096 | bytes 16384 | tf_op jit(solution)/shard_map/psum | solution.py:180
  575.4 52.5 %all-reduce.9.cloned.1.call-done = bf16[512,512]{0,1:T(8,128)(2,1)} async-done(((bf16[512,512]{0,1:T(8,128)(2,1)}), bf16[512,512]{0,1:T(8,128)(2,1)}) %all-reduce.9.cloned.1.call-update) | async-done | bytes 524304 | tf_op jit(solution)/shard_map/psum | solution.py:181
  635.2 37.5 %all-reduce.11.cloned.1.call-done = bf16[512,1024]{1,0:T(8,128)(2,1)} async-done(((bf16[512,1024]{1,0:T(8,128)(2,1)}), bf16[512,1024]{1,0:T(8,128)(2,1)}) %all-reduce.11.cloned.1.call-update) | async-done | bytes 1048592 | tf_op jit(solution)/shard_map/psum | solution.py:187
  (124 shorter events, 67.1 us)
Async XLA Ops:
  7.2 406.0 %copy-start = (bf16[1408,1024]{1,0:T(8,128)(2,1)S(1)}, bf16[1408,1024]{1,0:T(8,128)(2,1)}, u32[]{:S(2)}) copy-start(bf16[1408,1024]{1,0:T(8,128)(2,1)} %param.25) | copy-start | bytes 8650756
  7.2 4.1 copy-start.12
  7.2 140.1 %all-gather.2.cloned.1.call-start = ((), (), s32[]{:S(2)}) async-start(), calls=%async_computation | async-start | bytes 17825792 | tf_op jit(solution)/shard_map/all_gather | solution.py:109
  7.2 4.1 copy-start.3
  14.5 390.8 %all-reduce.5.cloned.1.call-start = ((), (), s32[]{:S(2)}) async-start(), calls=%async_computation.1 | async-start | bytes 2097152 | tf_op jit(solution)/shard_map/psum | solution.py:139
  17.0 141.9 %copy-start.8 = (s32[16]{0:T(128)S(1)}, s32[16]{0:T(128)}, u32[]{:S(2)}) copy-start(s32[16]{0:T(128)} %param.27) | copy-start | bytes 196
  178.6 15.0 %copy-start.1 = (f32[512,512]{0,1:T(8,128)S(1)}, f32[512,512]{0,1:T(8,128)}, u32[]{:S(2)}) copy-start(f32[512,512]{0,1:T(8,128)} %get-tuple-element.278) | copy-start | bytes 3145732 | tf_op jit(solution)/shard_map/while
  194.0 15.7 %copy-start.2 = (f32[512,512]{0,1:T(8,128)}, f32[512,512]{0,1:T(8,128)S(1)}, u32[]{:S(2)}) copy-start(f32[512,512]{0,1:T(8,128)S(1)} %bitcast_add_fusion.2) | copy-start | bytes 3145732 | tf_op jit(solution)/shard_map/while
  229.6 15.0 %copy-start.1 = (f32[512,512]{0,1:T(8,128)S(1)}, f32[512,512]{0,1:T(8,128)}, u32[]{:S(2)}) copy-start(f32[512,512]{0,1:T(8,128)} %get-tuple-element.278) | copy-start | bytes 3145732 | tf_op jit(solution)/shard_map/while
  244.9 15.7 %copy-start.2 = (f32[512,512]{0,1:T(8,128)}, f32[512,512]{0,1:T(8,128)S(1)}, u32[]{:S(2)}) copy-start(f32[512,512]{0,1:T(8,128)S(1)} %bitcast_add_fusion.2) | copy-start | bytes 3145732 | tf_op jit(solution)/shard_map/while
  280.5 15.0 %copy-start.1 = (f32[512,512]{0,1:T(8,128)S(1)}, f32[512,512]{0,1:T(8,128)}, u32[]{:S(2)}) copy-start(f32[512,512]{0,1:T(8,128)} %get-tuple-element.278) | copy-start | bytes 3145732 | tf_op jit(solution)/shard_map/while
  295.8 15.7 %copy-start.2 = (f32[512,512]{0,1:T(8,128)}, f32[512,512]{0,1:T(8,128)S(1)}, u32[]{:S(2)}) copy-start(f32[512,512]{0,1:T(8,128)S(1)} %bitcast_add_fusion.2) | copy-start | bytes 3145732 | tf_op jit(solution)/shard_map/while
  331.4 15.0 %copy-start.1 = (f32[512,512]{0,1:T(8,128)S(1)}, f32[512,512]{0,1:T(8,128)}, u32[]{:S(2)}) copy-start(f32[512,512]{0,1:T(8,128)} %get-tuple-element.278) | copy-start | bytes 3145732 | tf_op jit(solution)/shard_map/while
  346.8 15.7 %copy-start.2 = (f32[512,512]{0,1:T(8,128)}, f32[512,512]{0,1:T(8,128)S(1)}, u32[]{:S(2)}) copy-start(f32[512,512]{0,1:T(8,128)S(1)} %bitcast_add_fusion.2) | copy-start | bytes 3145732 | tf_op jit(solution)/shard_map/while
  363.9 43.4 %copy-start.13 = (f32[1024]{0:T(1024)S(1)}, f32[1024]{0:T(1024)}, u32[]{:S(2)}) copy-start(f32[1024]{0:T(1024)} %param.23) | copy-start | bytes 12292
  366.9 94.5 %all-reduce.7.cloned.1.call-start = ((), (), s32[]{:S(2)}) async-start(), calls=%async_computation.2 | async-start | bytes 2097152 | tf_op jit(solution)/shard_map/psum | solution.py:144
  413.2 9.6 %copy-start.14 = (f32[1024]{0:T(1024)S(1)}, f32[1024]{0:T(1024)}, u32[]{:S(2)}) copy-start(f32[1024]{0:T(1024)} %param.30) | copy-start | bytes 12292
  421.1 206.8 %all-reduce.9.cloned.1.call-start = ((), (), s32[]{:S(2)}) async-start(), calls=%async_computation.3 | async-start | bytes 1048576 | tf_op jit(solution)/shard_map/psum | solution.py:181
  422.8 41.1 %copy-start.10 = (f32[1024]{0:T(1024)S(1)}, f32[1024]{0:T(1024)}, u32[]{:S(2)}) copy-start(f32[1024]{0:T(1024)} %param.26) | copy-start | bytes 12292
  461.3 2.6 copy-start.4
  461.3 2.6 copy-start.5
  461.3 2.8 copy-start.6
  540.5 132.2 %all-reduce.11.cloned.1.call-start = ((), (), s32[]{:S(2)}) async-start(), calls=%async_computation.4 | async-start | bytes 2097152 | tf_op jit(solution)/shard_map/psum | solution.py:187
  545.2 86.8 %copy-start.9 = (s32[4]{0:T(128)S(1)}, s32[4]{0:T(128)}, u32[]{:S(2)}) copy-start(s32[4]{0:T(128)} %param.29) | copy-start | bytes 52
  (2 other events, 4.0 us)
Sparse Core Ops, SparseCore 0:
  14.6 132.6 all-gather.1
  367.0 38.2 all-reduce.4
  421.2 40.0 all-reduce.6
  540.6 87.1 all-reduce.8
  632.1 40.5 all-reduce.10
